TPU v7x, 32 devices: a whole 2x2x4 slice. The times are simulated.
32 devices in a mesh: pipe: 1, seq: 32 (over z, y, x, core).
Axes of the slice: x: 2, y: 2, z: 4, core: 2. Of those that a mesh axis runs over, the one named last changes fastest.
Arguments:
- inputs: bfloat16 [2, 16384, 512], P(None, 'seq'), may hold values from -6 to 6
- w_in: bfloat16 [1, 512, 2048], P('pipe'), may hold values from -0.25 to 0.25
- w_out: bfloat16 [1, 512, 512], P('pipe'), may hold values from -0.25 to 0.25
- lengths: int32 [2, 8], replicated, may hold values from 1 to 4096, 16384 in all within a row
- valid: int32 [2, 32], replicated, may hold values from 128 to 512
Outputs:
- states: bfloat16 [1, 2, 16384, 512], P('pipe', None, 'seq')
Inputs may be any that keep to these rules, and one draw needn't show every extreme that they name: Each row of stream lengths sums to 16384.
All inputs are finite; a program needn't handle non-finite values.
Results may differ from a plain program's by a relative error of at most 0.025.
Values may be sent and summed in bfloat16 or wider, within the bound.
A program may use at most 64 MiB of HBM per device.

v0:
```python
import functools
import math

import jax
import jax.numpy as jnp
from jax import lax
from jax.experimental import pallas as pl
from jax.experimental.pallas import tpu as pltpu
from jax.sharding import PartitionSpec as P

HEAD_DIM = 128
WINDOW = 512
TILE = 256
LANES = 128
PARTS = 3
HEADS_AT_ONCE = 4

norm_eps = 1e-05
out_eps = 0.001

score_scale = 1.0 / math.sqrt(HEAD_DIM)
mix_scale = 1.0 / math.sqrt(WINDOW)
fold = score_scale * mix_scale * 0.5
inner = 1.0 / mix_scale


def normalise(values, epsilon):
    mean = jnp.mean(values, axis=-1, keepdims=True)
    centred = values - mean
    spread = jnp.mean(centred * centred, axis=-1, keepdims=True)
    return centred * lax.rsqrt(spread + epsilon)


def silu(v):
    half = v * 0.5
    return half + half * jnp.tanh(half)


def layer_kernel(
    micro, size,
    x_hbm, win_hbm, wout_hbm, len_ref, val_ref, out_hbm,
    x_v, xr_v, win_v, wout_v, out_v, norm_v, u_v, v_v, q_v, k_v, kp_v, vp_v, acc_v, lo_v,
    load_sem, weight_sem, out_sem, send_sem, recv_sem,
):
    block = lax.axis_index("seq")
    tok, width = x_v.shape[1], x_v.shape[2]
    branch = wout_v.shape[0]
    heads = branch // HEAD_DIM
    streams = len_ref.shape[1]
    f32 = jnp.float32
    bf16 = jnp.bfloat16

    loads = [
        pltpu.make_async_copy(x_hbm.at[m], x_v.at[m], load_sem.at[m]) for m in range(micro)
    ]
    weights = [
        pltpu.make_async_copy(
            win_hbm.at[0, :, pl.ds(c * branch, branch)], win_v.at[c], weight_sem.at[c]
        )
        for c in range(4)
    ]
    weights.append(pltpu.make_async_copy(wout_hbm.at[0], wout_v, weight_sem.at[4]))
    for copy in loads + weights[:4]:
        copy.start()
    weights[4].start()

    def parts(m):
        half, quarter = tok // 2, tok // 4
        if m < micro - 1:
            return [(0, tok)]
        return [(half, tok), (quarter, half), (0, quarter)]

    def sends(m, p):
        first, last = parts(m)[p]
        rows = pl.ds(first, last - first)
        return pltpu.make_async_remote_copy(
            src_ref=x_v.at[m, rows, :],
            dst_ref=xr_v.at[m, rows, :],
            send_sem=send_sem.at[m, p],
            recv_sem=recv_sem.at[m, p],
            device_id={"seq": block + 1},
            device_id_type=pl.DeviceIdType.MESH,
        )

    def out_copy(m, p):
        first, last = parts(m)[p]
        rows = pl.ds(first, last - first)
        return pltpu.make_async_copy(
            out_v.at[m, rows, :], out_hbm.at[m, rows, :], out_sem.at[m, p]
        )

    barrier = pltpu.get_barrier_semaphore()

    @pl.when(block > 0)
    def _():
        pl.semaphore_signal(
            barrier, inc=1, device_id={"seq": block - 1}, device_id_type=pl.DeviceIdType.MESH
        )

    @pl.when(block < size - 1)
    def _():
        pl.semaphore_wait(barrier, 1)

    for m in range(micro):
        loads[m].wait()

        @pl.when(block < size - 1)
        def _():
            for p in range(len(parts(m))):
                sends(m, p).start()

    @pl.when(block == 0)
    def _():
        xr_v[...] = jnp.zeros_like(xr_v)

    row = lax.broadcasted_iota(jnp.int32, (tok, LANES), 0)
    for m in range(micro):
        place = row + block * tok
        start = jnp.zeros((tok, LANES), jnp.int32)
        bound = jnp.int32(0)
        for k in range(streams):
            bound = bound + len_ref[m, k]
            start = jnp.where(place >= bound, bound, start)
        lo_v[m] = start - block * tok

    def norm_rows(source, m, first=0, last=None):
        for at in range(first, tok if last is None else last, 128):
            rows = slice(at, at + 128)
            norm_v[rows, :] = normalise(source[m, rows, :].astype(f32), norm_eps).astype(bf16)

    live_row = lax.broadcasted_iota(jnp.int32, (tok, branch), 0)

    def project(c):
        return jnp.dot(norm_v[...], win_v[c], preferred_element_type=f32)

    def weigh(query, keys, keep):
        s = lax.dot_general(query, keys, (((1,), (1,)), ((), ())), preferred_element_type=f32)
        a = s + s * jnp.tanh(s * inner)
        return jnp.where(keep, a, 0.0).astype(bf16)

    def attend(m, previous, top=0, end=None):
        end = tok if end is None else end
        tile = min(TILE, end - top)
        key_ref, value_ref = (kp_v, vp_v) if previous else (k_v, v_v)

        def group(g, carry):
            plans = []
            for i in range(HEADS_AT_ONCE):
                cols = pl.ds(
                    pl.multiple_of((g * HEADS_AT_ONCE + i) * HEAD_DIM, HEAD_DIM), HEAD_DIM
                )
                for at in range(top, end, tile):
                    rows = slice(at, at + tile)
                    first, last = (at, tok) if previous else (0, at + tile)
                    span = slice(first, last)
                    shape = (tile, last - first)
                    low = jnp.concatenate([lo_v[m, rows, :]] * (shape[1] // LANES), 1)
                    place = lax.broadcasted_iota(jnp.int32, shape, 1) + first
                    line = lax.broadcasted_iota(jnp.int32, shape, 0) + at
                    if previous:
                        keep = (place - tok >= low) & (place > line)
                    else:
                        keep = (place >= low) & (place <= line)
                    plans.append((rows, cols, span, keep))
            parts = [weigh(q_v[m, r, c], key_ref[k, c], keep) for r, c, k, keep in plans]
            for (r, c, k, _), a in zip(plans, parts):
                part = jnp.dot(a, value_ref[k, c], preferred_element_type=f32)
                acc_v[m, r, c] = acc_v[m, r, c] + part if previous else part
            return carry

        lax.fori_loop(0, heads // HEADS_AT_ONCE, group, 0)

    for m in range(micro):
        norm_rows(x_v, m)
        count = val_ref[m, block]
        for c in range(4):
            if m == 0:
                weights[c].wait()
            part = silu(project(c))
            if c == 0:
                u_v[m] = part.astype(bf16)
            elif c == 1:
                v_v[...] = jnp.where(live_row < count, part, 0.0).astype(bf16)
            elif c == 2:
                q_v[m] = (part.astype(bf16).astype(f32) * fold).astype(bf16)
            else:
                k_v[...] = part.astype(bf16)
        attend(m, False)

    weights[4].wait()
    for m in range(micro):
        before = jnp.where(block > 0, val_ref[m, jnp.maximum(block - 1, 0)], 0)
        count = val_ref[m, block]
        for p in range(len(parts(m))):
            first, last = parts(m)[p]
            rows = slice(first, last)

            @pl.when(block > 0)
            def _():
                sends(m, p).wait_recv()

            norm_rows(xr_v, m, first, last)
            normed = norm_v[rows, :]
            value = silu(jnp.dot(normed, win_v[1], preferred_element_type=f32))
            vp_v[rows, :] = jnp.where(live_row[: last - first] + first < before, value, 0.0).astype(bf16)
            kp_v[rows, :] = silu(jnp.dot(normed, win_v[3], preferred_element_type=f32)).astype(bf16)
            attend(m, True, first, last)
            for at in range(first, last, 128):
                rows = slice(at, at + 128)
                gated = normalise(acc_v[m, rows, :], out_eps) * u_v[m, rows, :].astype(f32)
                gated = jnp.where(live_row[:128] + at < count, gated, 0.0).astype(bf16)
                out_v[m, rows, :] = (
                    x_v[m, rows, :].astype(f32)
                    + jnp.dot(gated, wout_v[...], preferred_element_type=f32)
                ).astype(bf16)
            out_copy(m, p).start()
    for m in range(micro):
        for p in range(len(parts(m))):
            out_copy(m, p).wait()

        @pl.when(block < size - 1)
        def _():
            for p in range(len(parts(m))):
                sends(m, p).wait_send()


def layer(x, w_in, w_out, lengths, valid):
    micro, tok, width = x.shape
    branch = w_out.shape[1]
    size = lax.axis_size("seq")
    assert tok == WINDOW
    bf16 = jnp.bfloat16
    anywhere = pl.BlockSpec(memory_space=pl.ANY)
    scalars = pl.BlockSpec(memory_space=pltpu.SMEM)
    return pl.pallas_call(
        functools.partial(layer_kernel, micro, size),
        out_shape=jax.ShapeDtypeStruct((micro, tok, width), bf16),
        in_specs=[anywhere, anywhere, anywhere, scalars, scalars],
        out_specs=anywhere,
        scratch_shapes=[
            pltpu.VMEM((micro, tok, width), bf16),
            pltpu.VMEM((micro, tok, width), bf16),
            pltpu.VMEM((4, width, branch), bf16),
            pltpu.VMEM((branch, width), bf16),
            pltpu.VMEM((micro, tok, width), bf16),
            pltpu.VMEM((tok, width), bf16),
            pltpu.VMEM((micro, tok, branch), bf16),
            pltpu.VMEM((tok, branch), bf16),
            pltpu.VMEM((micro, tok, branch), bf16),
            pltpu.VMEM((tok, branch), bf16),
            pltpu.VMEM((tok, branch), bf16),
            pltpu.VMEM((tok, branch), bf16),
            pltpu.VMEM((micro, tok, branch), jnp.float32),
            pltpu.VMEM((micro, tok, LANES), jnp.int32),
            pltpu.SemaphoreType.DMA((micro,)),
            pltpu.SemaphoreType.DMA((5,)),
            pltpu.SemaphoreType.DMA((micro, PARTS)),
            pltpu.SemaphoreType.DMA((micro, PARTS)),
            pltpu.SemaphoreType.DMA((micro, PARTS)),
        ],
        compiler_params=pltpu.CompilerParams(
            collective_id=0, has_side_effects=True, vmem_limit_bytes=56 * 1024 * 1024
        ),
    )(x, w_in, w_out, lengths, valid)


def shards(inputs, w_in, w_out, lengths, valid):
    micro, tok, width = inputs.shape
    sections = lax.axis_size("pipe")
    if sections == 1:
        return layer(inputs, w_in, w_out, lengths, valid)[None]

    section = lax.axis_index("pipe")
    pairs = [(i, i + 1) for i in range(sections - 1)]

    def tick(step, carry):
        incoming, states = carry
        slot = step - section
        active = (slot >= 0) & (slot < micro)
        index = jnp.clip(slot, 0, micro - 1)
        fresh = lax.dynamic_index_in_dim(inputs, index, 0, keepdims=True)
        x_rows = jnp.where(section == 0, fresh, incoming)
        result = layer(
            x_rows,
            w_in,
            w_out,
            lax.dynamic_index_in_dim(lengths, index, 0, keepdims=True),
            lax.dynamic_index_in_dim(valid, index, 0, keepdims=True),
        )
        zero = jnp.zeros((), jnp.int32)
        updated = lax.dynamic_update_slice(states, result[None], (zero, index, zero, zero))
        states = jnp.where(active, updated, states)
        return (lax.ppermute(result, "pipe", pairs), states)

    start = (
        jnp.zeros((1, tok, width), jnp.bfloat16),
        jnp.zeros((1, micro, tok, width), jnp.bfloat16),
    )
    return lax.fori_loop(0, sections + micro - 1, tick, start)[1]


def solution(mesh):
    in_specs = (P(None, "seq", None), P("pipe", None, None), P("pipe", None, None), P(), P())
    out_specs = P("pipe", None, "seq", None)
    return jax.shard_map(shards, mesh=mesh, in_specs=in_specs, out_specs=out_specs, check_vma=False)
```

profile of v0, /device:TPU:24, one launch (start us, length us, event | category | flops | bytes accessed | tf_op | source)
XLA Modules:
  0.0 21.1 jit_solution(13355416446730695212)
XLA Ops:
  0.0 18.9 %shard_map.55 = bf16[2,512,512]{2,1,0:T(8,128)(2,1)} custom-call(bf16[2,512,512]{2,1,0:T(8,128)(2,1)} %x_hbm.1, bf16[1,512,2048]{2,1,0:T(8,128)(2,1)} %win_hbm.1, bf16[1,512,512]{2,1,0:T(8,128)(2,1)} %wout_hbm.1, s32[2,8]{1,0:T(2,128)} %len_ref.1, s32[2,32]{1,0:T(2,128)} %val_ref.1), custom_call_target="tpu_custom_call" | custom-call | tf_op jit(solution)/shard_map/pallas_call | solution.py:235
  18.9 2.3 %copy.7 = bf16[1,2,512,512]{3,2,1,0:T(8,128)(2,1)} copy(bf16[1,2,512,512]{3,2,1,0:T(8,128)(2,1)} %bitcast.1) | data formatting | bytes 2097152
where the time goes:
time: 21.3 us; the launch traced here: 21.1 us
  Pallas kernels  18.9 us (89%)
  local copies, waits for them, and re-layouts  2.26 us (11%)
    pallas_call x1, Pallas kernels, layer(): pl.pallas_call(functools.partial(layer_kernel, micro, size), out_shape=ja...  18.9 us
    unnamed x1, local copies, waits for them, and re-layouts  2.26 us

commit v1 on v0

--- a/solution.py
+++ b/solution.py
@@ -38,11 +38,19 @@
 
 def layer_kernel(
     micro, size,
-    x_hbm, win_hbm, wout_hbm, len_ref, val_ref, out_hbm,
-    x_v, xr_v, win_v, wout_v, out_v, norm_v, u_v, v_v, q_v, k_v, kp_v, vp_v, acc_v, lo_v,
-    load_sem, weight_sem, out_sem, send_sem, recv_sem,
+    x_hbm, win_hbm, wout_hbm, len_hbm, val_hbm, out_v,
+    x_v, xr_v, win_v, wout_v, norm_v, u_v, v_v, q_v, k_v, kp_v, vp_v, acc_v, lo_v, len_ref, val_ref,
+    load_sem, weight_sem, scalar_sem, send_sem, recv_sem,
 ):
     block = lax.axis_index("seq")
+    barrier = pltpu.get_barrier_semaphore()
+
+    @pl.when(block > 0)
+    def _():
+        pl.semaphore_signal(
+            barrier, inc=1, device_id={"seq": block - 1}, device_id_type=pl.DeviceIdType.MESH
+        )
+
     tok, width = x_v.shape[1], x_v.shape[2]
     branch = wout_v.shape[0]
     heads = branch // HEAD_DIM
@@ -60,9 +68,12 @@
         for c in range(4)
     ]
     weights.append(pltpu.make_async_copy(wout_hbm.at[0], wout_v, weight_sem.at[4]))
-    for copy in loads + weights[:4]:
+    scalars = [
+        pltpu.make_async_copy(len_hbm, len_ref, scalar_sem.at[0]),
+        pltpu.make_async_copy(val_hbm, val_ref, scalar_sem.at[1]),
+    ]
+    for copy in loads + scalars + weights:
         copy.start()
-    weights[4].start()
 
     def parts(m):
         half, quarter = tok // 2, tok // 4
@@ -82,30 +93,13 @@
             device_id_type=pl.DeviceIdType.MESH,
         )
 
-    def out_copy(m, p):
-        first, last = parts(m)[p]
-        rows = pl.ds(first, last - first)
-        return pltpu.make_async_copy(
-            out_v.at[m, rows, :], out_hbm.at[m, rows, :], out_sem.at[m, p]
-        )
-
-    barrier = pltpu.get_barrier_semaphore()
-
-    @pl.when(block > 0)
-    def _():
-        pl.semaphore_signal(
-            barrier, inc=1, device_id={"seq": block - 1}, device_id_type=pl.DeviceIdType.MESH
-        )
-
-    @pl.when(block < size - 1)
-    def _():
-        pl.semaphore_wait(barrier, 1)
-
     for m in range(micro):
         loads[m].wait()
 
         @pl.when(block < size - 1)
         def _():
+            if m == 0:
+                pl.semaphore_wait(barrier, 1)
             for p in range(len(parts(m))):
                 sends(m, p).start()
 
@@ -113,6 +107,8 @@
     def _():
         xr_v[...] = jnp.zeros_like(xr_v)
 
+    for copy in scalars:
+        copy.wait()
     row = lax.broadcasted_iota(jnp.int32, (tok, LANES), 0)
     for m in range(micro):
         place = row + block * tok
@@ -213,11 +209,7 @@
                     x_v[m, rows, :].astype(f32)
                     + jnp.dot(gated, wout_v[...], preferred_element_type=f32)
                 ).astype(bf16)
-            out_copy(m, p).start()
-    for m in range(micro):
-        for p in range(len(parts(m))):
-            out_copy(m, p).wait()
-
+    for m in range(micro):
         @pl.when(block < size - 1)
         def _():
             for p in range(len(parts(m))):
@@ -231,18 +223,16 @@
     assert tok == WINDOW
     bf16 = jnp.bfloat16
     anywhere = pl.BlockSpec(memory_space=pl.ANY)
-    scalars = pl.BlockSpec(memory_space=pltpu.SMEM)
     return pl.pallas_call(
         functools.partial(layer_kernel, micro, size),
-        out_shape=jax.ShapeDtypeStruct((micro, tok, width), bf16),
-        in_specs=[anywhere, anywhere, anywhere, scalars, scalars],
-        out_specs=anywhere,
+        out_shape=pltpu.VMEM((micro, tok, width), bf16),
+        in_specs=[anywhere] * 5,
+        out_specs=pl.BlockSpec(memory_space=pltpu.VMEM),
         scratch_shapes=[
             pltpu.VMEM((micro, tok, width), bf16),
             pltpu.VMEM((micro, tok, width), bf16),
             pltpu.VMEM((4, width, branch), bf16),
             pltpu.VMEM((branch, width), bf16),
-            pltpu.VMEM((micro, tok, width), bf16),
             pltpu.VMEM((tok, width), bf16),
             pltpu.VMEM((micro, tok, branch), bf16),
             pltpu.VMEM((tok, branch), bf16),
@@ -252,9 +242,11 @@
             pltpu.VMEM((tok, branch), bf16),
             pltpu.VMEM((micro, tok, branch), jnp.float32),
             pltpu.VMEM((micro, tok, LANES), jnp.int32),
+            pltpu.SMEM(lengths.shape, jnp.int32),
+            pltpu.SMEM(valid.shape, jnp.int32),
             pltpu.SemaphoreType.DMA((micro,)),
             pltpu.SemaphoreType.DMA((5,)),
-            pltpu.SemaphoreType.DMA((micro, PARTS)),
+            pltpu.SemaphoreType.DMA((2,)),
             pltpu.SemaphoreType.DMA((micro, PARTS)),
             pltpu.SemaphoreType.DMA((micro, PARTS)),
         ],

time: 21.3 us -> 18.6 us (0.87)
  Pallas kernels: 18.9 us -> 17.4 us
  local copies, waits for them, and re-layouts: 2.26 us -> 0.97 us
    pallas_call x1, Pallas kernels: 18.9 us -> 17.4 us  [layer(): pl.pallas_call(functools.partial(layer_kernel, micro, size), out_shape=pl...]
    unnamed x1, local copies, waits for them, and re-layouts: 2.26 us -> 0.97 us
where the time goes in v1:
time: 18.6 us; the launch traced here: 18.4 us
  Pallas kernels  17.4 us (94%)
  local copies, waits for them, and re-layouts  0.97 us (5%)
    pallas_call x1, Pallas kernels, layer(): pl.pallas_call(functools.partial(layer_kernel, micro, size), out_shape=pl...  17.4 us
    unnamed x1, local copies, waits for them, and re-layouts  0.97 us

profile of v1, /device:TPU:24, one launch (start us, length us, event | category | flops | bytes accessed | tf_op | source)
XLA Modules:
  0.0 18.4 jit_solution(5495546151302766201)
XLA Ops:
  0.0 17.4 %shard_map.55 = bf16[2,512,512]{2,1,0:T(8,128)(2,1)S(1)} custom-call(bf16[2,512,512]{2,1,0:T(8,128)(2,1)} %x_hbm.1, bf16[1,512,2048]{2,1,0:T(8,128)(2,1)} %win_hbm.1, bf16[1,512,512]{2,1,0:T(8,128)(2,1)} %wout_hbm.1, s32[2,8]{1,0:T(2,128)} %len_hbm.1, s32[2,32]{1,0:T(2,128)} %val_hbm.1), custom_call_target="tpu_custom_call" | custom-call | tf_op jit(solution)/shard_map/pallas_call | solution.py:226
  17.5 1.0 %copy.7 = bf16[1,2,512,512]{3,2,1,0:T(8,128)(2,1)} copy(bf16[1,2,512,512]{3,2,1,0:T(8,128)(2,1)S(1)} %bitcast.1) | data formatting | bytes 2097152

commit v2 on v1

--- a/solution.py
+++ b/solution.py
@@ -13,15 +13,15 @@
 TILE = 256
 LANES = 128
 PARTS = 3
-HEADS_AT_ONCE = 4
+PLANE = 8
+DETOUR = 80
 
 norm_eps = 1e-05
 out_eps = 0.001
 
 score_scale = 1.0 / math.sqrt(HEAD_DIM)
-mix_scale = 1.0 / math.sqrt(WINDOW)
-fold = score_scale * mix_scale * 0.5
-inner = 1.0 / mix_scale
+fold = score_scale * 0.5
+mixed_eps = out_eps * WINDOW
 
 
 def normalise(values, epsilon):
@@ -37,19 +37,29 @@
 
 
 def layer_kernel(
-    micro, size,
+    micro, size, detours,
     x_hbm, win_hbm, wout_hbm, len_hbm, val_hbm, out_v,
-    x_v, xr_v, win_v, wout_v, norm_v, u_v, v_v, q_v, k_v, kp_v, vp_v, acc_v, lo_v, len_ref, val_ref,
-    load_sem, weight_sem, scalar_sem, send_sem, recv_sem,
+    x_v, xr_v, win_v, wout_v, norm_v, u_v, v_v, q_v, k_v, kp_v, vp_v, acc_v, lo_v, len_ref, val_ref, detour_v,
+    load_sem, weight_sem, scalar_sem, send_sem, recv_sem, detour_sem,
 ):
     block = lax.axis_index("seq")
     barrier = pltpu.get_barrier_semaphore()
 
-    @pl.when(block > 0)
-    def _():
-        pl.semaphore_signal(
-            barrier, inc=1, device_id={"seq": block - 1}, device_id_type=pl.DeviceIdType.MESH
-        )
+    def greet(when, device):
+        @pl.when(when)
+        def _():
+            pl.semaphore_signal(
+                barrier, inc=1, device_id={"seq": device}, device_id_type=pl.DeviceIdType.MESH
+            )
+
+    greet(block > 0, block - 1)
+    detour_of = [
+        (z * PLANE + PLANE - 1, 0, z * PLANE + PLANE, z * DETOUR)
+        for z in range(detours)
+    ]
+    for source, via, target, _ in detour_of:
+        greet(block == target, via)
+        greet(block == via, source)
 
     tok, width = x_v.shape[1], x_v.shape[2]
     branch = wout_v.shape[0]
@@ -78,36 +88,94 @@
     def parts(m):
         half, quarter = tok // 2, tok // 4
         if m < micro - 1:
-            return [(0, tok)]
+            return [(half, tok), (0, half)]
         return [(half, tok), (quarter, half), (0, quarter)]
 
-    def sends(m, p):
+    def remote(src, dst, send, recv, device):
+        return pltpu.make_async_remote_copy(
+            src_ref=src,
+            dst_ref=dst,
+            send_sem=send,
+            recv_sem=recv,
+            device_id={"seq": device},
+            device_id_type=pl.DeviceIdType.MESH,
+        )
+
+    def sends(m, p, cut=0):
         first, last = parts(m)[p]
-        rows = pl.ds(first, last - first)
-        return pltpu.make_async_remote_copy(
-            src_ref=x_v.at[m, rows, :],
-            dst_ref=xr_v.at[m, rows, :],
-            send_sem=send_sem.at[m, p],
-            recv_sem=recv_sem.at[m, p],
-            device_id={"seq": block + 1},
-            device_id_type=pl.DeviceIdType.MESH,
-        )
-
-    for m in range(micro):
-        loads[m].wait()
-
-        @pl.when(block < size - 1)
-        def _():
-            if m == 0:
+        rows = pl.ds(first, last - cut - first)
+        return remote(
+            x_v.at[m, rows, :], xr_v.at[m, rows, :], send_sem.at[m, p], recv_sem.at[m, p], block + 1
+        )
+
+    final = micro - 1
+
+    def leave(via, slot):
+        rows = pl.ds(tok - DETOUR, DETOUR)
+        return remote(
+            x_v.at[final, rows, :], detour_v.at[pl.ds(slot, DETOUR), :],
+            detour_sem.at[0], detour_sem.at[1 + slot // DETOUR], via,
+        )
+
+    def forward(target, slot):
+        rows = pl.ds(tok - DETOUR, DETOUR)
+        return remote(
+            detour_v.at[pl.ds(slot, DETOUR), :], xr_v.at[final, rows, :],
+            detour_sem.at[1 + detours + slot // DETOUR], detour_sem.at[1 + 2 * detours], target,
+        )
+
+    def route(when, m, p, act, end):
+        plain = when
+        if (m, p) == (final, 0):
+            for source, via, target, slot in detour_of:
+                here = block == (source if end == 0 else target)
+                plain = plain & jnp.logical_not(here)
+
+                @pl.when(here)
+                def _():
+                    act(sends(m, p, DETOUR))
+                    if end:
+                        act(forward(target, slot))
+
+        @pl.when(plain)
+        def _():
+            act(sends(m, p))
+
+    early = block < size - 1
+    if detours:
+        early = early & (block > 0)
+
+    for m in range(micro):
+        if m == 0:
+            for copy in loads:
+                copy.wait()
+            one = early
+            for source, _, _, _ in detour_of:
+                one = one & (block != source)
+
+                @pl.when(block == source)
+                def _():
+                    pl.semaphore_wait(barrier, 2)
+
+            @pl.when(one)
+            def _():
                 pl.semaphore_wait(barrier, 1)
-            for p in range(len(parts(m))):
-                sends(m, p).start()
+
+            for source, via, _, slot in detour_of:
+                @pl.when(block == source)
+                def _():
+                    leave(via, slot).start()
+
+        if m == final:
+            pass
+        for p in range(len(parts(m))):
+            route(early, m, p, lambda copy: copy.start(), 0)
 
     @pl.when(block == 0)
     def _():
         xr_v[...] = jnp.zeros_like(xr_v)
 
-    for copy in scalars:
+    for copy in scalars + weights:
         copy.wait()
     row = lax.broadcasted_iota(jnp.int32, (tok, LANES), 0)
     for m in range(micro):
@@ -129,49 +197,37 @@
     def project(c):
         return jnp.dot(norm_v[...], win_v[c], preferred_element_type=f32)
 
+    def mask(m, previous, at, end, first, last):
+        shape = (end - at, last - first)
+        low = jnp.concatenate([lo_v[m, at:end, :]] * (shape[1] // LANES), 1)
+        place = lax.broadcasted_iota(jnp.int32, shape, 1) + (first - tok if previous else first)
+        keep = place >= low
+        line = lax.broadcasted_iota(jnp.int32, shape, 0) + at
+        if previous:
+            return keep & (place > line - tok) if first < end else keep
+        return keep & (place <= line) if last > at else keep
+
     def weigh(query, keys, keep):
         s = lax.dot_general(query, keys, (((1,), (1,)), ((), ())), preferred_element_type=f32)
-        a = s + s * jnp.tanh(s * inner)
-        return jnp.where(keep, a, 0.0).astype(bf16)
-
-    def attend(m, previous, top=0, end=None):
-        end = tok if end is None else end
-        tile = min(TILE, end - top)
+        return jnp.where(keep, s + s * jnp.tanh(s), 0.0).astype(bf16)
+
+    def attend(m, previous, blocks):
         key_ref, value_ref = (kp_v, vp_v) if previous else (k_v, v_v)
-
-        def group(g, carry):
-            plans = []
-            for i in range(HEADS_AT_ONCE):
-                cols = pl.ds(
-                    pl.multiple_of((g * HEADS_AT_ONCE + i) * HEAD_DIM, HEAD_DIM), HEAD_DIM
-                )
-                for at in range(top, end, tile):
-                    rows = slice(at, at + tile)
-                    first, last = (at, tok) if previous else (0, at + tile)
-                    span = slice(first, last)
-                    shape = (tile, last - first)
-                    low = jnp.concatenate([lo_v[m, rows, :]] * (shape[1] // LANES), 1)
-                    place = lax.broadcasted_iota(jnp.int32, shape, 1) + first
-                    line = lax.broadcasted_iota(jnp.int32, shape, 0) + at
-                    if previous:
-                        keep = (place - tok >= low) & (place > line)
-                    else:
-                        keep = (place >= low) & (place <= line)
-                    plans.append((rows, cols, span, keep))
-            parts = [weigh(q_v[m, r, c], key_ref[k, c], keep) for r, c, k, keep in plans]
-            for (r, c, k, _), a in zip(plans, parts):
-                part = jnp.dot(a, value_ref[k, c], preferred_element_type=f32)
-                acc_v[m, r, c] = acc_v[m, r, c] + part if previous else part
-            return carry
-
-        lax.fori_loop(0, heads // HEADS_AT_ONCE, group, 0)
+        plans = []
+        for h in range(heads):
+            cols = slice(h * HEAD_DIM, (h + 1) * HEAD_DIM)
+            for at, end, first, last in blocks:
+                keep = mask(m, previous, at, end, first, last)
+                plans.append((slice(at, end), cols, slice(first, last), keep))
+        weights = [weigh(q_v[m, r, c], key_ref[k, c], keep) for r, c, k, keep in plans]
+        for (r, c, k, _), a in zip(plans, weights):
+            part = jnp.dot(a, value_ref[k, c], preferred_element_type=f32)
+            acc_v[m, r, c] = acc_v[m, r, c] + part if previous else part
 
     for m in range(micro):
         norm_rows(x_v, m)
         count = val_ref[m, block]
         for c in range(4):
-            if m == 0:
-                weights[c].wait()
             part = silu(project(c))
             if c == 0:
                 u_v[m] = part.astype(bf16)
@@ -181,39 +237,63 @@
                 q_v[m] = (part.astype(bf16).astype(f32) * fold).astype(bf16)
             else:
                 k_v[...] = part.astype(bf16)
-        attend(m, False)
-
-    weights[4].wait()
+        attend(m, False, [(at, at + TILE, 0, at + TILE) for at in range(0, tok, TILE)])
+
+    if detours:
+        @pl.when(block == 0)
+        def _():
+            pl.semaphore_wait(barrier, 1 + detours)
+            for m in range(micro):
+                for p in range(len(parts(m))):
+                    sends(m, p).start()
+            for _, _, target, slot in detour_of:
+                leave(0, slot).wait_recv()
+                forward(target, slot).start()
+
+    def finish(m, first, last):
+        count = val_ref[m, block]
+        for at in range(first, last, 128):
+            rows = slice(at, at + 128)
+            gated = normalise(acc_v[m, rows, :], mixed_eps) * u_v[m, rows, :].astype(f32)
+            gated = jnp.where(live_row[:128] + at < count, gated, 0.0).astype(bf16)
+            out_v[m, rows, :] = (
+                x_v[m, rows, :].astype(f32)
+                + jnp.dot(gated, wout_v[...], preferred_element_type=f32)
+            ).astype(bf16)
+
+    ready = []
     for m in range(micro):
         before = jnp.where(block > 0, val_ref[m, jnp.maximum(block - 1, 0)], 0)
-        count = val_ref[m, block]
         for p in range(len(parts(m))):
             first, last = parts(m)[p]
             rows = slice(first, last)
 
-            @pl.when(block > 0)
-            def _():
-                sends(m, p).wait_recv()
+            route(block > 0, m, p, lambda copy: copy.wait_recv(), 1)
 
             norm_rows(xr_v, m, first, last)
             normed = norm_v[rows, :]
             value = silu(jnp.dot(normed, win_v[1], preferred_element_type=f32))
             vp_v[rows, :] = jnp.where(live_row[: last - first] + first < before, value, 0.0).astype(bf16)
             kp_v[rows, :] = silu(jnp.dot(normed, win_v[3], preferred_element_type=f32)).astype(bf16)
-            attend(m, True, first, last)
-            for at in range(first, last, 128):
-                rows = slice(at, at + 128)
-                gated = normalise(acc_v[m, rows, :], out_eps) * u_v[m, rows, :].astype(f32)
-                gated = jnp.where(live_row[:128] + at < count, gated, 0.0).astype(bf16)
-                out_v[m, rows, :] = (
-                    x_v[m, rows, :].astype(f32)
-                    + jnp.dot(gated, wout_v[...], preferred_element_type=f32)
-                ).astype(bf16)
-    for m in range(micro):
-        @pl.when(block < size - 1)
-        def _():
-            for p in range(len(parts(m))):
-                sends(m, p).wait_send()
+            ahead = [(at, min(at + TILE, first), first, last) for at in range(0, first, TILE)]
+            own = [(at, min(at + TILE, last), at, last) for at in range(first, last, TILE)]
+            attend(m, True, own + ahead)
+            for done in ready:
+                finish(*done)
+            ready = [(m, first, last)]
+    for done in ready:
+        finish(*done)
+    for m in range(micro):
+        for p in range(len(parts(m))):
+            route(block < size - 1, m, p, lambda copy: copy.wait_send(), 0)
+    for source, via, target, slot in detour_of:
+        @pl.when(block == source)
+        def _():
+            leave(via, slot).wait_send()
+
+        @pl.when(block == via)
+        def _():
+            forward(target, slot).wait_send()
 
 
 def layer(x, w_in, w_out, lengths, valid):
@@ -221,10 +301,12 @@
     branch = w_out.shape[1]
     size = lax.axis_size("seq")
     assert tok == WINDOW
+    planes = size // PLANE if lax.axis_size("pipe") == 1 else 0
+    detours = max(planes - 1, 0)
     bf16 = jnp.bfloat16
     anywhere = pl.BlockSpec(memory_space=pl.ANY)
     return pl.pallas_call(
-        functools.partial(layer_kernel, micro, size),
+        functools.partial(layer_kernel, micro, size, detours),
         out_shape=pltpu.VMEM((micro, tok, width), bf16),
         in_specs=[anywhere] * 5,
         out_specs=pl.BlockSpec(memory_space=pltpu.VMEM),
@@ -244,11 +326,13 @@
             pltpu.VMEM((micro, tok, LANES), jnp.int32),
             pltpu.SMEM(lengths.shape, jnp.int32),
             pltpu.SMEM(valid.shape, jnp.int32),
+            pltpu.VMEM((DETOUR * max(detours, 1), width), bf16),
             pltpu.SemaphoreType.DMA((micro,)),
             pltpu.SemaphoreType.DMA((5,)),
             pltpu.SemaphoreType.DMA((2,)),
             pltpu.SemaphoreType.DMA((micro, PARTS)),
             pltpu.SemaphoreType.DMA((micro, PARTS)),
+            pltpu.SemaphoreType.DMA((2 + 2 * detours,)),
         ],
         compiler_params=pltpu.CompilerParams(
             collective_id=0, has_side_effects=True, vmem_limit_bytes=56 * 1024 * 1024

time: 18.6 us -> 17.8 us (0.957)
  Pallas kernels: 17.4 us -> 16.7 us
    pallas_call x1, Pallas kernels: 17.4 us -> 16.7 us  [layer(): pl.pallas_call(functools.partial(layer_kernel, micro, size, detours), out...]
where the time goes in v2:
time: 17.8 us; the launch traced here: 17.7 us
  Pallas kernels  16.7 us (94%)
  local copies, waits for them, and re-layouts  0.97 us (5%)
    pallas_call x1, Pallas kernels, layer(): pl.pallas_call(functools.partial(layer_kernel, micro, size, detours), out...  16.7 us
    unnamed x1, local copies, waits for them, and re-layouts  0.97 us

profile of v2, /device:TPU:24, one launch (start us, length us, event | category | flops | bytes accessed | tf_op | source)
XLA Modules:
  0.0 17.7 jit_solution(16446714181856611627)
XLA Ops:
  0.0 16.7 %shard_map.55 = bf16[2,512,512]{2,1,0:T(8,128)(2,1)S(1)} custom-call(bf16[2,512,512]{2,1,0:T(8,128)(2,1)} %x_hbm.1, bf16[1,512,2048]{2,1,0:T(8,128)(2,1)} %win_hbm.1, bf16[1,512,512]{2,1,0:T(8,128)(2,1)} %wout_hbm.1, s32[2,8]{1,0:T(2,128)} %len_hbm.1, s32[2,32]{1,0:T(2,128)} %val_hbm.1), custom_call_target="tpu_custom_call" | custom-call | tf_op jit(solution)/shard_map/pallas_call | solution.py:308
  16.7 1.0 %copy.7 = bf16[1,2,512,512]{3,2,1,0:T(8,128)(2,1)} copy(bf16[1,2,512,512]{3,2,1,0:T(8,128)(2,1)S(1)} %bitcast.1) | data formatting | bytes 2097152

commit v3 on v2

--- a/solution.py
+++ b/solution.py
@@ -39,7 +39,7 @@
 def layer_kernel(
     micro, size, detours,
     x_hbm, win_hbm, wout_hbm, len_hbm, val_hbm, out_v,
-    x_v, xr_v, win_v, wout_v, norm_v, u_v, v_v, q_v, k_v, kp_v, vp_v, acc_v, lo_v, len_ref, val_ref, detour_v,
+    x_v, xr_v, win_v, wout_v, norm_v, u_v, v_v, q_v, k_v, kp_v, vp_v, acc_v, lo_v, len_ref, val_ref, detour_v, sum_v, gain_v,
     load_sem, weight_sem, scalar_sem, send_sem, recv_sem, detour_sem,
 ):
     block = lax.axis_index("seq")
@@ -147,8 +147,7 @@
 
     for m in range(micro):
         if m == 0:
-            for copy in loads:
-                copy.wait()
+            loads[0].wait()
             one = early
             for source, _, _, _ in detour_of:
                 one = one & (block != source)
@@ -161,13 +160,17 @@
             def _():
                 pl.semaphore_wait(barrier, 1)
 
+
+        if m == final:
+            pass
+        if m > 0:
+            loads[m].wait()
+        if m == final:
             for source, via, _, slot in detour_of:
                 @pl.when(block == source)
                 def _():
                     leave(via, slot).start()
 
-        if m == final:
-            pass
         for p in range(len(parts(m))):
             route(early, m, p, lambda copy: copy.start(), 0)
 
@@ -193,6 +196,10 @@
             norm_v[rows, :] = normalise(source[m, rows, :].astype(f32), norm_eps).astype(bf16)
 
     live_row = lax.broadcasted_iota(jnp.int32, (tok, branch), 0)
+
+    for c in (1, 3):
+        ones = jnp.ones((8, width), bf16)
+        sum_v[c] = jnp.dot(ones, win_v[c], preferred_element_type=f32)
 
     def project(c):
         return jnp.dot(norm_v[...], win_v[c], preferred_element_type=f32)
@@ -227,7 +234,7 @@
     for m in range(micro):
         norm_rows(x_v, m)
         count = val_ref[m, block]
-        for c in range(4):
+        for c in (2, 3, 1, 0):
             part = silu(project(c))
             if c == 0:
                 u_v[m] = part.astype(bf16)
@@ -250,6 +257,38 @@
                 leave(0, slot).wait_recv()
                 forward(target, slot).start()
 
+    def raw_projection(rows):
+        raw = rows.astype(f32)
+        mean = jnp.mean(raw, axis=-1, keepdims=True)
+        centred = raw - mean
+        scale = lax.rsqrt(jnp.mean(centred * centred, axis=-1, keepdims=True) + norm_eps)
+
+        def part(c):
+            product = jnp.dot(rows, win_v[c], preferred_element_type=f32)
+            return scale * (product - mean * sum_v[c, 0:1, :])
+
+        return part
+
+    def prepare(m, last):
+        rows = slice(0, last)
+        acc = acc_v[m, rows, :]
+        acc_v[m, rows, :] = acc - jnp.mean(acc, axis=-1, keepdims=True)
+        gain_v[...] = jnp.dot(u_v[m, rows, :], wout_v[...], preferred_element_type=f32)
+
+    def finish_last(m, last):
+        rows = slice(0, last)
+        acc = acc_v[m, rows, :]
+        product = jnp.dot(
+            (acc * u_v[m, rows, :].astype(f32)).astype(bf16), wout_v[...], preferred_element_type=f32
+        )
+        mean = jnp.mean(acc, axis=-1, keepdims=True)
+        centred = acc - mean
+        scale = lax.rsqrt(jnp.mean(centred * centred, axis=-1, keepdims=True) + mixed_eps)
+        mixed = jnp.where(
+            live_row[:last, :1] < val_ref[m, block], scale * (product - mean * gain_v[...]), 0.0
+        )
+        out_v[m, rows, :] = (x_v[m, rows, :].astype(f32) + mixed).astype(bf16)
+
     def finish(m, first, last):
         count = val_ref[m, block]
         for at in range(first, last, 128):
@@ -261,6 +300,20 @@
                 + jnp.dot(gated, wout_v[...], preferred_element_type=f32)
             ).astype(bf16)
 
+    def settle():
+        for m in range(micro):
+            for p in range(len(parts(m))):
+                if (m, p) != (final, len(parts(final)) - 1):
+                    route(block < size - 1, m, p, lambda copy: copy.wait_send(), 0)
+        for source, via, target, slot in detour_of:
+            @pl.when(block == source)
+            def _():
+                leave(via, slot).wait_send()
+
+            @pl.when(block == via)
+            def _():
+                forward(target, slot).wait_send()
+
     ready = []
     for m in range(micro):
         before = jnp.where(block > 0, val_ref[m, jnp.maximum(block - 1, 0)], 0)
@@ -268,32 +321,32 @@
             first, last = parts(m)[p]
             rows = slice(first, last)
 
+            if (m, first) == (final, 0):
+                settle()
             route(block > 0, m, p, lambda copy: copy.wait_recv(), 1)
 
-            norm_rows(xr_v, m, first, last)
-            normed = norm_v[rows, :]
-            value = silu(jnp.dot(normed, win_v[1], preferred_element_type=f32))
+            if (m, first) == (final, 0):
+                remote_part = raw_projection(xr_v[m, rows, :])
+            else:
+                norm_rows(xr_v, m, first, last)
+                normed = norm_v[rows, :]
+
+                def remote_part(c):
+                    return jnp.dot(normed, win_v[c], preferred_element_type=f32)
+
+            kp_v[rows, :] = silu(remote_part(3)).astype(bf16)
+            value = silu(remote_part(1))
             vp_v[rows, :] = jnp.where(live_row[: last - first] + first < before, value, 0.0).astype(bf16)
-            kp_v[rows, :] = silu(jnp.dot(normed, win_v[3], preferred_element_type=f32)).astype(bf16)
             ahead = [(at, min(at + TILE, first), first, last) for at in range(0, first, TILE)]
             own = [(at, min(at + TILE, last), at, last) for at in range(first, last, TILE)]
             attend(m, True, own + ahead)
             for done in ready:
                 finish(*done)
             ready = [(m, first, last)]
-    for done in ready:
-        finish(*done)
-    for m in range(micro):
-        for p in range(len(parts(m))):
-            route(block < size - 1, m, p, lambda copy: copy.wait_send(), 0)
-    for source, via, target, slot in detour_of:
-        @pl.when(block == source)
-        def _():
-            leave(via, slot).wait_send()
-
-        @pl.when(block == via)
-        def _():
-            forward(target, slot).wait_send()
+            if m == final and p == len(parts(m)) - 2:
+                prepare(m, first)
+    finish_last(final, tok // 4)
+    route(block < size - 1, final, len(parts(final)) - 1, lambda copy: copy.wait_send(), 0)
 
 
 def layer(x, w_in, w_out, lengths, valid):
@@ -327,6 +380,8 @@
             pltpu.SMEM(lengths.shape, jnp.int32),
             pltpu.SMEM(valid.shape, jnp.int32),
             pltpu.VMEM((DETOUR * max(detours, 1), width), bf16),
+            pltpu.VMEM((4, 8, branch), jnp.float32),
+            pltpu.VMEM((tok // 4, width), jnp.float32),
             pltpu.SemaphoreType.DMA((micro,)),
             pltpu.SemaphoreType.DMA((5,)),
             pltpu.SemaphoreType.DMA((2,)),

time: 17.8 us -> 17.4 us (0.978)
  Pallas kernels: 16.7 us -> 16.3 us
    pallas_call x1, Pallas kernels: 16.7 us -> 16.3 us  [layer(): pl.pallas_call(functools.partial(layer_kernel, micro, size, detours), out...]
where the time goes in v3:
time: 17.4 us; the launch traced here: 17.3 us
  Pallas kernels  16.3 us (94%)
  local copies, waits for them, and re-layouts  0.97 us (6%)
    pallas_call x1, Pallas kernels, layer(): pl.pallas_call(functools.partial(layer_kernel, micro, size, detours), out...  16.3 us
    unnamed x1, local copies, waits for them, and re-layouts  0.97 us

profile of v3, /device:TPU:24, one launch (start us, length us, event | category | flops | bytes accessed | tf_op | source)
XLA Modules:
  0.0 17.3 jit_solution(13362552583892842255)
XLA Ops:
  0.0 16.3 %shard_map.55 = bf16[2,512,512]{2,1,0:T(8,128)(2,1)S(1)} custom-call(bf16[2,512,512]{2,1,0:T(8,128)(2,1)} %x_hbm.1, bf16[1,512,2048]{2,1,0:T(8,128)(2,1)} %win_hbm.1, bf16[1,512,512]{2,1,0:T(8,128)(2,1)} %wout_hbm.1, s32[2,8]{1,0:T(2,128)} %len_hbm.1, s32[2,32]{1,0:T(2,128)} %val_hbm.1), custom_call_target="tpu_custom_call" | custom-call | tf_op jit(solution)/shard_map/pallas_call | solution.py:361
  16.3 1.0 %copy.7 = bf16[1,2,512,512]{3,2,1,0:T(8,128)(2,1)} copy(bf16[1,2,512,512]{3,2,1,0:T(8,128)(2,1)S(1)} %bitcast.1) | data formatting | bytes 2097152

commit v4 on v3

--- a/solution.py
+++ b/solution.py
@@ -15,6 +15,7 @@
 PARTS = 3
 PLANE = 8
 DETOUR = 80
+VMEM_LIMIT = 40 * 1024 * 1024
 
 norm_eps = 1e-05
 out_eps = 0.001
@@ -36,10 +37,29 @@
     return half + half * jnp.tanh(half)
 
 
+def mask(low, previous, at, end, first, last, tok):
+    shape = (end - at, last - first)
+    low = jnp.concatenate([low] * (shape[1] // LANES), 1)
+    place = lax.broadcasted_iota(jnp.int32, shape, 1) + (first - tok if previous else first)
+    keep = place >= low
+    line = lax.broadcasted_iota(jnp.int32, shape, 0) + at
+    if previous:
+        return keep & (place > line - tok) if first < end else keep
+    return keep & (place <= line) if last > at else keep
+
+
+def weigh(query, keys, keep):
+    s = lax.dot_general(
+        query, keys, (((1,), (1,)), ((), ())), preferred_element_type=jnp.float32
+    )
+    return jnp.where(keep, s + s * jnp.tanh(s), 0.0).astype(jnp.bfloat16)
+
+
 def layer_kernel(
     micro, size, detours,
-    x_hbm, win_hbm, wout_hbm, len_hbm, val_hbm, out_v,
-    x_v, xr_v, win_v, wout_v, norm_v, u_v, v_v, q_v, k_v, kp_v, vp_v, acc_v, lo_v, len_ref, val_ref, detour_v, sum_v, gain_v,
+    x_hbm, win_hbm, wout_hbm, len_hbm, val_hbm,
+    out_v, x_v, win_v, wout_v, u_v, q_v, acc_v, lo_v, sum_v, gain_v, last_v, live_v,
+    xr_v, norm_v, v_v, k_v, kp_v, vp_v, len_ref, val_ref, detour_v,
     load_sem, weight_sem, scalar_sem, send_sem, recv_sem, detour_sem,
 ):
     block = lax.axis_index("seq")
@@ -204,27 +224,13 @@
     def project(c):
         return jnp.dot(norm_v[...], win_v[c], preferred_element_type=f32)
 
-    def mask(m, previous, at, end, first, last):
-        shape = (end - at, last - first)
-        low = jnp.concatenate([lo_v[m, at:end, :]] * (shape[1] // LANES), 1)
-        place = lax.broadcasted_iota(jnp.int32, shape, 1) + (first - tok if previous else first)
-        keep = place >= low
-        line = lax.broadcasted_iota(jnp.int32, shape, 0) + at
-        if previous:
-            return keep & (place > line - tok) if first < end else keep
-        return keep & (place <= line) if last > at else keep
-
-    def weigh(query, keys, keep):
-        s = lax.dot_general(query, keys, (((1,), (1,)), ((), ())), preferred_element_type=f32)
-        return jnp.where(keep, s + s * jnp.tanh(s), 0.0).astype(bf16)
-
     def attend(m, previous, blocks):
         key_ref, value_ref = (kp_v, vp_v) if previous else (k_v, v_v)
         plans = []
         for h in range(heads):
             cols = slice(h * HEAD_DIM, (h + 1) * HEAD_DIM)
             for at, end, first, last in blocks:
-                keep = mask(m, previous, at, end, first, last)
+                keep = mask(lo_v[m, at:end, :], previous, at, end, first, last, tok)
                 plans.append((slice(at, end), cols, slice(first, last), keep))
         weights = [weigh(q_v[m, r, c], key_ref[k, c], keep) for r, c, k, keep in plans]
         for (r, c, k, _), a in zip(plans, weights):
@@ -257,37 +263,11 @@
                 leave(0, slot).wait_recv()
                 forward(target, slot).start()
 
-    def raw_projection(rows):
-        raw = rows.astype(f32)
-        mean = jnp.mean(raw, axis=-1, keepdims=True)
-        centred = raw - mean
-        scale = lax.rsqrt(jnp.mean(centred * centred, axis=-1, keepdims=True) + norm_eps)
-
-        def part(c):
-            product = jnp.dot(rows, win_v[c], preferred_element_type=f32)
-            return scale * (product - mean * sum_v[c, 0:1, :])
-
-        return part
-
     def prepare(m, last):
         rows = slice(0, last)
         acc = acc_v[m, rows, :]
         acc_v[m, rows, :] = acc - jnp.mean(acc, axis=-1, keepdims=True)
         gain_v[...] = jnp.dot(u_v[m, rows, :], wout_v[...], preferred_element_type=f32)
-
-    def finish_last(m, last):
-        rows = slice(0, last)
-        acc = acc_v[m, rows, :]
-        product = jnp.dot(
-            (acc * u_v[m, rows, :].astype(f32)).astype(bf16), wout_v[...], preferred_element_type=f32
-        )
-        mean = jnp.mean(acc, axis=-1, keepdims=True)
-        centred = acc - mean
-        scale = lax.rsqrt(jnp.mean(centred * centred, axis=-1, keepdims=True) + mixed_eps)
-        mixed = jnp.where(
-            live_row[:last, :1] < val_ref[m, block], scale * (product - mean * gain_v[...]), 0.0
-        )
-        out_v[m, rows, :] = (x_v[m, rows, :].astype(f32) + mixed).astype(bf16)
 
     def finish(m, first, last):
         count = val_ref[m, block]
@@ -323,19 +303,20 @@
 
             if (m, first) == (final, 0):
                 settle()
+                lane_row = lax.broadcasted_iota(jnp.int32, (last, LANES), 0)
+                for slot, limit in enumerate((before, val_ref[m, block], val_ref[m, block] - last)):
+                    live_v[slot] = (lane_row < limit).astype(jnp.int32)
             route(block > 0, m, p, lambda copy: copy.wait_recv(), 1)
-
             if (m, first) == (final, 0):
-                remote_part = raw_projection(xr_v[m, rows, :])
-            else:
-                norm_rows(xr_v, m, first, last)
-                normed = norm_v[rows, :]
-
-                def remote_part(c):
-                    return jnp.dot(normed, win_v[c], preferred_element_type=f32)
-
-            kp_v[rows, :] = silu(remote_part(3)).astype(bf16)
-            value = silu(remote_part(1))
+                last_v[...] = xr_v[m, rows, :]
+                break
+
+            norm_rows(xr_v, m, first, last)
+            normed = norm_v[rows, :]
+            kp_v[rows, :] = silu(
+                jnp.dot(normed, win_v[3], preferred_element_type=f32)
+            ).astype(bf16)
+            value = silu(jnp.dot(normed, win_v[1], preferred_element_type=f32))
             vp_v[rows, :] = jnp.where(live_row[: last - first] + first < before, value, 0.0).astype(bf16)
             ahead = [(at, min(at + TILE, first), first, last) for at in range(0, first, TILE)]
             own = [(at, min(at + TILE, last), at, last) for at in range(first, last, TILE)]
@@ -345,8 +326,70 @@
             ready = [(m, first, last)]
             if m == final and p == len(parts(m)) - 2:
                 prepare(m, first)
-    finish_last(final, tok // 4)
     route(block < size - 1, final, len(parts(final)) - 1, lambda copy: copy.wait_send(), 0)
+
+
+def tail_kernel(
+    done_v, x_v, win_v, wout_v, u_v, q_v, acc_v, lo_v, sum_v, gain_v, last_v, live_v, out_hbm,
+    tail_v, key_v, value_v, sem,
+):
+    micro, tok, width = x_v.shape
+    m, last = micro - 1, last_v.shape[0]
+    heads = wout_v.shape[0] // HEAD_DIM
+    f32 = jnp.float32
+    bf16 = jnp.bfloat16
+    copies = [
+        pltpu.make_async_copy(done_v.at[i], out_hbm.at[i], sem.at[i]) for i in range(m)
+    ]
+    rest = pl.ds(2 * last, tok - 2 * last)
+    copies.append(pltpu.make_async_copy(done_v.at[m, rest, :], out_hbm.at[m, rest, :], sem.at[m]))
+    for copy in copies:
+        copy.start()
+
+    def live(slot):
+        return jnp.concatenate([live_v[slot]] * (width // LANES), 1) > 0
+
+    raw = last_v[...].astype(f32)
+    mean = jnp.mean(raw, axis=-1, keepdims=True)
+    centred = raw - mean
+    scale = lax.rsqrt(jnp.mean(centred * centred, axis=-1, keepdims=True) + norm_eps)
+
+    def remote_part(c):
+        product = jnp.dot(last_v[...], win_v[c], preferred_element_type=f32)
+        return silu(scale * (product - mean * sum_v[c, 0:1, :]))
+
+    key_v[...] = remote_part(3).astype(bf16)
+    value_v[...] = jnp.where(live(0), remote_part(1), 0.0).astype(bf16)
+    rows = slice(0, last)
+    keep = mask(lo_v[m, rows, :], True, 0, last, 0, last, tok)
+    columns = [slice(h * HEAD_DIM, (h + 1) * HEAD_DIM) for h in range(heads)]
+    weights = [weigh(q_v[m, rows, c], key_v[:, c], keep) for c in columns]
+    parts = [
+        acc_v[m, rows, c] + jnp.dot(a, value_v[:, c], preferred_element_type=f32)
+        for c, a in zip(columns, weights)
+    ]
+
+    after = slice(last, 2 * last)
+    gated = normalise(acc_v[m, after, :], mixed_eps) * u_v[m, after, :].astype(f32)
+    gated = jnp.where(live(2), gated, 0.0).astype(bf16)
+    tail_v[after, :] = (
+        x_v[m, after, :].astype(f32) + jnp.dot(gated, wout_v[...], preferred_element_type=f32)
+    ).astype(bf16)
+
+    acc = jnp.concatenate(parts, 1)
+    product = jnp.dot(
+        (acc * u_v[m, rows, :].astype(f32)).astype(bf16), wout_v[...], preferred_element_type=f32
+    )
+    middle = jnp.mean(acc, axis=-1, keepdims=True)
+    centred = acc - middle
+    spread = lax.rsqrt(jnp.mean(centred * centred, axis=-1, keepdims=True) + mixed_eps)
+    mixed = jnp.where(live(1), spread * (product - middle * gain_v[...]), 0.0)
+    tail_v[rows, :] = (x_v[m, rows, :].astype(f32) + mixed).astype(bf16)
+    head = pl.ds(0, 2 * last)
+    copies.append(pltpu.make_async_copy(tail_v, out_hbm.at[m, head, :], sem.at[micro]))
+    copies[-1].start()
+    for copy in copies:
+        copy.wait()
 
 
 def layer(x, w_in, w_out, lengths, valid):
@@ -357,31 +400,39 @@
     planes = size // PLANE if lax.axis_size("pipe") == 1 else 0
     detours = max(planes - 1, 0)
     bf16 = jnp.bfloat16
+    f32 = jnp.float32
     anywhere = pl.BlockSpec(memory_space=pl.ANY)
-    return pl.pallas_call(
+    local = pl.BlockSpec(memory_space=pltpu.VMEM)
+    last = tok // 4
+    kept = [
+        pltpu.VMEM((micro, tok, width), bf16),
+        pltpu.VMEM((micro, tok, width), bf16),
+        pltpu.VMEM((4, width, branch), bf16),
+        pltpu.VMEM((branch, width), bf16),
+        pltpu.VMEM((micro, tok, branch), bf16),
+        pltpu.VMEM((micro, tok, branch), bf16),
+        pltpu.VMEM((micro, tok, branch), f32),
+        pltpu.VMEM((micro, tok, LANES), jnp.int32),
+        pltpu.VMEM((4, 8, branch), f32),
+        pltpu.VMEM((last, width), f32),
+        pltpu.VMEM((last, width), bf16),
+        pltpu.VMEM((3, last, LANES), jnp.int32),
+    ]
+    state = pl.pallas_call(
         functools.partial(layer_kernel, micro, size, detours),
-        out_shape=pltpu.VMEM((micro, tok, width), bf16),
+        out_shape=kept,
         in_specs=[anywhere] * 5,
-        out_specs=pl.BlockSpec(memory_space=pltpu.VMEM),
+        out_specs=[local] * len(kept),
         scratch_shapes=[
             pltpu.VMEM((micro, tok, width), bf16),
-            pltpu.VMEM((micro, tok, width), bf16),
-            pltpu.VMEM((4, width, branch), bf16),
-            pltpu.VMEM((branch, width), bf16),
             pltpu.VMEM((tok, width), bf16),
-            pltpu.VMEM((micro, tok, branch), bf16),
-            pltpu.VMEM((tok, branch), bf16),
-            pltpu.VMEM((micro, tok, branch), bf16),
             pltpu.VMEM((tok, branch), bf16),
             pltpu.VMEM((tok, branch), bf16),
             pltpu.VMEM((tok, branch), bf16),
-            pltpu.VMEM((micro, tok, branch), jnp.float32),
-            pltpu.VMEM((micro, tok, LANES), jnp.int32),
+            pltpu.VMEM((tok, branch), bf16),
             pltpu.SMEM(lengths.shape, jnp.int32),
             pltpu.SMEM(valid.shape, jnp.int32),
             pltpu.VMEM((DETOUR * max(detours, 1), width), bf16),
-            pltpu.VMEM((4, 8, branch), jnp.float32),
-            pltpu.VMEM((tok // 4, width), jnp.float32),
             pltpu.SemaphoreType.DMA((micro,)),
             pltpu.SemaphoreType.DMA((5,)),
             pltpu.SemaphoreType.DMA((2,)),
@@ -390,9 +441,25 @@
             pltpu.SemaphoreType.DMA((2 + 2 * detours,)),
         ],
         compiler_params=pltpu.CompilerParams(
-            collective_id=0, has_side_effects=True, vmem_limit_bytes=56 * 1024 * 1024
+            collective_id=0, has_side_effects=True, vmem_limit_bytes=VMEM_LIMIT
         ),
-    )(x, w_in, w_out, lengths, valid)
+    )(*[
+        pltpu.with_memory_space_constraint(array, pltpu.HBM)
+        for array in (x, w_in, w_out, lengths, valid)
+    ])
+    return pl.pallas_call(
+        tail_kernel,
+        out_shape=jax.ShapeDtypeStruct((micro, tok, width), bf16),
+        in_specs=[local] * len(kept),
+        out_specs=anywhere,
+        scratch_shapes=[
+            pltpu.VMEM((2 * last, width), bf16),
+            pltpu.VMEM((last, branch), bf16),
+            pltpu.VMEM((last, branch), bf16),
+            pltpu.SemaphoreType.DMA((micro + 1,)),
+        ],
+        compiler_params=pltpu.CompilerParams(vmem_limit_bytes=VMEM_LIMIT),
+    )(*[pltpu.with_memory_space_constraint(array, pltpu.VMEM) for array in state])
 
 
 def shards(inputs, w_in, w_out, lengths, valid):

time: 17.4 us -> 17.2 us (0.989)
  local copies, waits for them, and re-layouts: 0.97 us -> 0 us
  Pallas kernels: 16.3 us -> 17.1 us
    pallas_call x0 -> x1, Pallas kernels: none -> 1.65 us  [layer(): pl.pallas_call(tail_kernel, out_shape=jax.ShapeDtypeStruct((micro, tok, w...]
    unnamed x1 -> x0, local copies, waits for them, and re-layouts: 0.97 us -> none
    pallas_call x1, Pallas kernels: 16.3 us -> 15.4 us  [layer(): pl.pallas_call(functools.partial(layer_kernel, micro, size, detours), out...]
where the time goes in v4:
time: 17.2 us; the launch traced here: 17.1 us
  Pallas kernels  17.1 us (99%)
    pallas_call x1, Pallas kernels, layer(): pl.pallas_call(functools.partial(layer_kernel, micro, size, detours), out...  15.4 us
    pallas_call x1, Pallas kernels, layer(): pl.pallas_call(tail_kernel, out_shape=jax.ShapeDtypeStruct((micro, tok, w...  1.65 us

profile of v4, /device:TPU:24, one launch (start us, length us, event | category | flops | bytes accessed | tf_op | source)
XLA Modules:
  0.0 17.1 jit_solution(17729641203504742712)
XLA Ops:
  0.0 15.4 %shard_map.55 = (bf16[2,512,512]{2,1,0:T(8,128)(2,1)S(1)}, bf16[2,512,512]{2,1,0:T(8,128)(2,1)S(1)}, bf16[4,512,512]{2,1,0:T(8,128)(2,1)S(1)}, bf16[512,512]{1,0...) custom-call(bf16[2,512,512]{2,1,0:T(8,128)(2,1)} %x_hbm.1, ...), custom_call_target="tpu_custom_call" | custom-call | tf_op jit(solution)/shard_map/pallas_call | solution.py:421
  15.4 1.6 %shard_map.56 = bf16[2,512,512]{2,1,0:T(8,128)(2,1)} custom-call(bf16[2,512,512]{2,1,0:T(8,128)(2,1)S(1)} %get-tuple-element.17.done_v, bf16[2,512,512]{2,1,0:T(8,128)(2,1)S(1)} %get-tuple-element.18.x_v, bf16[4,512,512]{2,1,0:T(8,128)(2,1)S(1)} %get-tuple-element.19.win_v, bf16[512,512]{1,0:T(8,128)(2,1)S(1)} %get-tuple-element.20.wout_v, ...), custom_call_target="tpu_custom_call" | custom-call | tf_op jit(solution)/shard_map/pallas_call | solution.py:450

commit v5 on v4

--- a/solution.py
+++ b/solution.py
@@ -304,7 +304,7 @@
             if (m, first) == (final, 0):
                 settle()
                 lane_row = lax.broadcasted_iota(jnp.int32, (last, LANES), 0)
-                for slot, limit in enumerate((before, val_ref[m, block], val_ref[m, block] - last)):
+                for slot, limit in enumerate((before, val_ref[m, block])):
                     live_v[slot] = (lane_row < limit).astype(jnp.int32)
             route(block > 0, m, p, lambda copy: copy.wait_recv(), 1)
             if (m, first) == (final, 0):
@@ -326,6 +326,7 @@
             ready = [(m, first, last)]
             if m == final and p == len(parts(m)) - 2:
                 prepare(m, first)
+                finish(*ready[0])
     route(block < size - 1, final, len(parts(final)) - 1, lambda copy: copy.wait_send(), 0)
 
 
@@ -341,7 +342,7 @@
     copies = [
         pltpu.make_async_copy(done_v.at[i], out_hbm.at[i], sem.at[i]) for i in range(m)
     ]
-    rest = pl.ds(2 * last, tok - 2 * last)
+    rest = pl.ds(last, tok - last)
     copies.append(pltpu.make_async_copy(done_v.at[m, rest, :], out_hbm.at[m, rest, :], sem.at[m]))
     for copy in copies:
         copy.start()
@@ -369,13 +370,6 @@
         for c, a in zip(columns, weights)
     ]
 
-    after = slice(last, 2 * last)
-    gated = normalise(acc_v[m, after, :], mixed_eps) * u_v[m, after, :].astype(f32)
-    gated = jnp.where(live(2), gated, 0.0).astype(bf16)
-    tail_v[after, :] = (
-        x_v[m, after, :].astype(f32) + jnp.dot(gated, wout_v[...], preferred_element_type=f32)
-    ).astype(bf16)
-
     acc = jnp.concatenate(parts, 1)
     product = jnp.dot(
         (acc * u_v[m, rows, :].astype(f32)).astype(bf16), wout_v[...], preferred_element_type=f32
@@ -384,8 +378,8 @@
     centred = acc - middle
     spread = lax.rsqrt(jnp.mean(centred * centred, axis=-1, keepdims=True) + mixed_eps)
     mixed = jnp.where(live(1), spread * (product - middle * gain_v[...]), 0.0)
-    tail_v[rows, :] = (x_v[m, rows, :].astype(f32) + mixed).astype(bf16)
-    head = pl.ds(0, 2 * last)
+    tail_v[...] = (x_v[m, rows, :].astype(f32) + mixed).astype(bf16)
+    head = pl.ds(0, last)
     copies.append(pltpu.make_async_copy(tail_v, out_hbm.at[m, head, :], sem.at[micro]))
     copies[-1].start()
     for copy in copies:
@@ -416,7 +410,7 @@
         pltpu.VMEM((4, 8, branch), f32),
         pltpu.VMEM((last, width), f32),
         pltpu.VMEM((last, width), bf16),
-        pltpu.VMEM((3, last, LANES), jnp.int32),
+        pltpu.VMEM((2, last, LANES), jnp.int32),
     ]
     state = pl.pallas_call(
         functools.partial(layer_kernel, micro, size, detours),
@@ -453,7 +447,7 @@
         in_specs=[local] * len(kept),
         out_specs=anywhere,
         scratch_shapes=[
-            pltpu.VMEM((2 * last, width), bf16),
+            pltpu.VMEM((last, width), bf16),
             pltpu.VMEM((last, branch), bf16),
             pltpu.VMEM((last, branch), bf16),
             pltpu.SemaphoreType.DMA((micro + 1,)),

time: 17.2 us -> 17.1 us (level)
  Pallas kernels: 17.1 us -> 16.9 us
where the time goes in v5:
time: 17.1 us; the launch traced here: 16.9 us
  Pallas kernels  16.9 us (99%)
    pallas_call x1, Pallas kernels, layer(): pl.pallas_call(functools.partial(layer_kernel, micro, size, detours), out...  15.4 us
    pallas_call x1, Pallas kernels, layer(): pl.pallas_call(tail_kernel, out_shape=jax.ShapeDtypeStruct((micro, tok, w...  1.52 us

profile of v5, /device:TPU:24, one launch (start us, length us, event | category | flops | bytes accessed | tf_op | source)
XLA Modules:
  0.0 16.9 jit_solution(5665599996573021806)
XLA Ops:
  0.0 15.4 %shard_map.55 = (bf16[2,512,512]{2,1,0:T(8,128)(2,1)S(1)}, bf16[2,512,512]{2,1,0:T(8,128)(2,1)S(1)}, bf16[4,512,512]{2,1,0:T(8,128)(2,1)S(1)}, bf16[512,512]{1,0...) custom-call(bf16[2,512,512]{2,1,0:T(8,128)(2,1)} %x_hbm.1, ...), custom_call_target="tpu_custom_call" | custom-call | tf_op jit(solution)/shard_map/pallas_call | solution.py:415
  15.4 1.5 %shard_map.56 = bf16[2,512,512]{2,1,0:T(8,128)(2,1)} custom-call(bf16[2,512,512]{2,1,0:T(8,128)(2,1)S(1)} %get-tuple-element.17.done_v, bf16[2,512,512]{2,1,0:T(8,128)(2,1)S(1)} %get-tuple-element.18.x_v, bf16[4,512,512]{2,1,0:T(8,128)(2,1)S(1)} %get-tuple-element.19.win_v, bf16[512,512]{1,0:T(8,128)(2,1)S(1)} %get-tuple-element.20.wout_v, ...), custom_call_target="tpu_custom_call" | custom-call | tf_op jit(solution)/shard_map/pallas_call | solution.py:444

commit v6 on v5

--- a/solution.py
+++ b/solution.py
@@ -14,7 +14,7 @@
 LANES = 128
 PARTS = 3
 PLANE = 8
-DETOUR = 80
+DETOUR = 96
 VMEM_LIMIT = 40 * 1024 * 1024
 
 norm_eps = 1e-05
@@ -375,8 +375,8 @@
         (acc * u_v[m, rows, :].astype(f32)).astype(bf16), wout_v[...], preferred_element_type=f32
     )
     middle = jnp.mean(acc, axis=-1, keepdims=True)
-    centred = acc - middle
-    spread = lax.rsqrt(jnp.mean(centred * centred, axis=-1, keepdims=True) + mixed_eps)
+    square = jnp.mean(acc * acc, axis=-1, keepdims=True) - middle * middle
+    spread = lax.rsqrt(jnp.maximum(square, 0.0) + mixed_eps)
     mixed = jnp.where(live(1), spread * (product - middle * gain_v[...]), 0.0)
     tail_v[...] = (x_v[m, rows, :].astype(f32) + mixed).astype(bf16)
     head = pl.ds(0, last)

time: 17.1 us -> 17 us (level)
  Pallas kernels: 16.9 us -> 16.7 us
    pallas_call x1, Pallas kernels: 15.4 us -> 15.2 us  [layer(): pl.pallas_call(functools.partial(layer_kernel, micro, size, detours), out...]
where the time goes in v6:
time: 17 us; the launch traced here: 16.7 us
  Pallas kernels  16.7 us (98%)
    pallas_call x1, Pallas kernels, layer(): pl.pallas_call(functools.partial(layer_kernel, micro, size, detours), out...  15.2 us
    pallas_call x1, Pallas kernels, layer(): pl.pallas_call(tail_kernel, out_shape=jax.ShapeDtypeStruct((micro, tok, w...  1.49 us

profile of v6, /device:TPU:24, one launch (start us, length us, event | category | flops | bytes accessed | tf_op | source)
XLA Modules:
  0.0 16.7 jit_solution(7991398261838505870)
XLA Ops:
  0.0 15.2 %shard_map.55 = (bf16[2,512,512]{2,1,0:T(8,128)(2,1)S(1)}, bf16[2,512,512]{2,1,0:T(8,128)(2,1)S(1)}, bf16[4,512,512]{2,1,0:T(8,128)(2,1)S(1)}, bf16[512,512]{1,0...) custom-call(bf16[2,512,512]{2,1,0:T(8,128)(2,1)} %x_hbm.1, ...), custom_call_target="tpu_custom_call" | custom-call | tf_op jit(solution)/shard_map/pallas_call | solution.py:415
  15.2 1.5 %shard_map.56 = bf16[2,512,512]{2,1,0:T(8,128)(2,1)} custom-call(bf16[2,512,512]{2,1,0:T(8,128)(2,1)S(1)} %get-tuple-element.17.done_v, bf16[2,512,512]{2,1,0:T(8,128)(2,1)S(1)} %get-tuple-element.18.x_v, bf16[4,512,512]{2,1,0:T(8,128)(2,1)S(1)} %get-tuple-element.19.win_v, bf16[512,512]{1,0:T(8,128)(2,1)S(1)} %get-tuple-element.20.wout_v, ...), custom_call_target="tpu_custom_call" | custom-call | tf_op jit(solution)/shard_map/pallas_call | solution.py:444
